TPU v7x, 256 devices: a whole 4x4x8 slice. The times are simulated.
256 devices in a mesh: ep: 8 (over y, core), fsdp: 32 (over z, x).
Axes of the slice: x: 4, y: 4, z: 8, core: 2. Of those that a mesh axis runs over, the one named last changes fastest.
Arguments:
- w_down: float32 [16, 6400, 4096], P('ep', None, 'fsdp'), may hold values from -0.15625 to 0.15625
- router_weight: float32 [4096, 16], P('fsdp', 'ep'), may hold values from -0.09375 to 0.09375
- router_gain: float32 [4096], P('fsdp'), may hold values from 0.25 to 1.75
Outputs:
- serve_down: bfloat16 [16, 6400, 4096], P('ep', 'fsdp')
- scale_down: float32 [16, 6400], P('ep', 'fsdp')
- serve_router: bfloat16 [4096, 16], replicated
All inputs are finite; a program needn't handle non-finite values.
Results may differ from a plain program's by a relative error of at most 0.001.
Values may be sent and summed in bfloat16 or wider, within the bound.
A program may use at most 64 MiB of HBM per device.

v0:
```python
import jax
import jax.numpy as jnp
from jax import lax
from jax.sharding import Mesh
from jax.sharding import PartitionSpec as P

FSDP = ("fsdp_0", "fsdp_1")


def by_axis(array, axes):
    for axis in axes:
        array = lax.psum(array, axis)
    return array


def in_order(parts, dim):
    lengths = list(parts.shape[1:])
    lengths[dim] *= parts.shape[0]
    return jnp.moveaxis(parts, 0, dim).reshape(lengths)


def copy_for_each(array, axis):
    size = lax.axis_size(axis)
    return lax.all_to_all(
        jnp.broadcast_to(array[None], (size, *array.shape)), axis, 0, 0, tiled=True
    )


def gather_directly(array, axis, dim):
    return in_order(copy_for_each(array, axis), dim)


def body(w_down, router_weight, router_gain):
    total_down = by_axis(jnp.sum(w_down * w_down, axis=2), FSDP)
    scale_down = jnp.sqrt(total_down)
    narrow_down = (w_down / jnp.expand_dims(scale_down, 2)).astype(jnp.bfloat16)
    serve_down = lax.all_to_all(narrow_down, FSDP, split_axis=1, concat_axis=2, tiled=True)
    scale_down = lax.dynamic_slice_in_dim(
        scale_down, lax.axis_index(FSDP) * serve_down.shape[1], serve_down.shape[1], axis=1
    )
    part_router = (router_weight * router_gain[:, None]).astype(jnp.bfloat16)
    row_router = gather_directly(part_router, FSDP, 0)
    serve_router = lax.all_gather(row_router, "ep", axis=1, tiled=True)
    return (serve_down, scale_down, serve_router)


def solution(mesh):
    split = Mesh(mesh.devices.reshape(mesh.shape["ep"], 8, 4), ("ep", "fsdp_0", "fsdp_1"))
    return jax.shard_map(
        body,
        mesh=split,
        in_specs=(P("ep", None, FSDP), P(FSDP, "ep"), P(FSDP)),
        out_specs=(P("ep", FSDP, None), P("ep", FSDP), P()),
        check_vma=False,
    )
```

profile of v0, /device:TPU:8, one launch (start us, length us, event | category | flops | bytes accessed | tf_op | source)
XLA Modules:
  0.0 177.8 jit_solution(15432574918795712005)
XLA Ops:
  0.6 0.7 multiply_convert_fusion
  1.3 0.6 broadcast_in_dim.2
  1.9 11.3 %all-to-all-start.1 = ((bf16[32,128,2]{1,2,0:T(2,128)(2,1)}), bf16[32,128,2]{1,2,0:T(2,128)(2,1)S(1)}, u32[]{:S(2)}, u32[]{:S(2)}) async-start(bf16[32,128,2]{1,2,0:T(2,128)(2,1)} %broadcast_in_dim.2), calls=%async_computation.1 | async-start | bytes 32768 | tf_op jit(solution)/shard_map/all_to_all | solution.py:24
  13.3 4.6 %multiply_reduce_fusion = f32[2,6400]{1,0:T(2,128)S(1)} fusion(f32[2,6400,128]{2,1,0:T(8,128)} %param.3), kind=kLoop, calls=%fused_computation.1 | loop fusion | flops 3264000 | bytes 6604800 | tf_op jit(solution)/shard_map/reduce_sum | solution.py:34
  17.9 30.5 %psum.14 = f32[2,6400]{1,0:T(2,128)S(1)} all-reduce(f32[2,6400]{1,0:T(2,128)S(1)} %multiply_reduce_fusion), channel_id=1, replica_groups=mesh['ep'=8,'fsdp_0'=8,'fsdp_1'=4] {'fsdp_0'}, use_global_device_ids=true, to_apply=%region_1.0 | all-reduce | flops 12800 | bytes 102400 | tf_op jit(solution)/shard_map/psum | solution.py:12
  48.4 17.4 %psum.15 = f32[2,6400]{1,0:T(2,128)S(1)} all-reduce(f32[2,6400]{1,0:T(2,128)S(1)} %psum.14), channel_id=1, replica_groups=mesh['ep'=8,'fsdp_0'=8,'fsdp_1'=4] {'fsdp_1'}, use_global_device_ids=true, to_apply=%region_2.0 | all-reduce | flops 12800 | bytes 102400 | tf_op jit(solution)/shard_map/psum | solution.py:12
  65.8 0.1 sqrt.3
  65.9 4.7 %divide_convert_fusion = bf16[2,6400,128]{2,1,0:T(8,128)(2,1)S(1)} fusion(f32[2,6400,128]{2,1,0:T(8,128)} %param.3, f32[2,6400]{1,0:T(2,128)S(1)} %sqrt.3), kind=kLoop, calls=%fused_computation | loop fusion | flops 3276800 | bytes 9881600 | tf_op jit(solution)/shard_map/convert_element_type | solution.py:36
  70.6 27.9 %copy.10 = bf16[2,6400,128]{2,0,1:T(2,128)(2,1)} copy(bf16[2,6400,128]{2,1,0:T(8,128)(2,1)S(1)} %divide_convert_fusion) | data formatting | bytes 6553600 | tf_op jit(solution)/shard_map/convert_element_type | solution.py:36
  98.5 0.0 all-to-all-done.1
  98.5 5.7 %all-to-all-start = ((bf16[2,6400,128]{2,0,1:T(2,128)(2,1)}), bf16[2,6400,128]{2,0,1:T(2,128)(2,1)S(1)}, u32[]{:S(2)}, u32[]{:S(2)}) async-start(bf16[2,6400,128]{2,0,1:T(2,128)(2,1)} %copy.10), calls=%async_computation | async-start | bytes 6553600 | tf_op jit(solution)/shard_map/all_to_all | solution.py:37
  104.2 0.7 constant_dynamic-slice_fusion
  104.9 12.9 %all-gather = bf16[8,2,4096]{2,1,0:T(2,128)(2,1)S(1)} all-gather(bf16[1,2,4096]{2,1,0:T(2,128)(2,1)S(1)} %bitcast.13), channel_id=1, replica_groups=mesh['ep'=8,'fsdp_0'=8,'fsdp_1'=4] {'ep'}, dimensions={0}, use_global_device_ids=true | all-gather | bytes 147456 | tf_op jit(solution)/shard_map/all_gather | solution.py:43
  117.8 0.7 reshape.14
  118.5 50.5 %all-to-all-done = bf16[2,6400,128]{2,0,1:T(2,128)(2,1)S(1)} async-done(((bf16[2,6400,128]{2,0,1:T(2,128)(2,1)}), bf16[2,6400,128]{2,0,1:T(2,128)(2,1)S(1)}, u32[]{:S(2)}, u32[]{:S(2)}) %all-to-all-start) | async-done | bytes 3276832 | tf_op jit(solution)/shard_map/all_to_all | solution.py:37
  169.1 2.5 %copy.11 = bf16[2,200,32,128]{3,2,1,0:T(8,128)(2,1)} copy(bf16[2,200,32,128]{3,0,1,2:T(2,128)(2,1)S(1)} %bitcast.11) | data formatting | bytes 6553600 | tf_op jit(solution)/shard_map/all_to_all | solution.py:37
  171.6 6.2 %all_to_all.19 = bf16[2,200,4096]{2,1,0:T(8,128)(2,1)} reshape(bf16[2,200,32,128]{3,2,1,0:T(8,128)(2,1)} %copy.11) | data formatting | bytes 6553600 | tf_op jit(solution)/shard_map/all_to_all | solution.py:37
Async XLA Ops:
  1.9 96.6 %all-to-all-start.1 = ((bf16[32,128,2]{1,2,0:T(2,128)(2,1)}), bf16[32,128,2]{1,2,0:T(2,128)(2,1)S(1)}, u32[]{:S(2)}, u32[]{:S(2)}) async-start(bf16[32,128,2]{1,2,0:T(2,128)(2,1)} %broadcast_in_dim.2), calls=%async_computation.1 | async-start | bytes 32768 | tf_op jit(solution)/shard_map/all_to_all | solution.py:24
  98.5 70.6 %all-to-all-start = ((bf16[2,6400,128]{2,0,1:T(2,128)(2,1)}), bf16[2,6400,128]{2,0,1:T(2,128)(2,1)S(1)}, u32[]{:S(2)}, u32[]{:S(2)}) async-start(bf16[2,6400,128]{2,0,1:T(2,128)(2,1)} %copy.10), calls=%async_computation | async-start | bytes 6553600 | tf_op jit(solution)/shard_map/all_to_all | solution.py:37
where the time goes:
time: 178 us
  blocking collectives  60.9 us (34%)
  waiting for transfers between devices  50.5 us (28%)
  local copies, waits for them, and re-layouts  38.6 us (22%)
  starting transfers between devices  17 us (10%)
  other arithmetic  10 us (6%)
    all_to_all x1, waiting for transfers between devices, body(): lax.all_to_all(narrow_down, FSDP, split_axis=1, concat_axis=2, tiled=True)  50.5 us
    psum x2, blocking collectives, by_axis(): array = lax.psum(array, axis)  47.9 us
    convert_element_type x1, local copies, waits for them, and re-layouts, body(): narrow_down = (w_down / jnp.expand_dims(scale_down, 2)).astype(jnp.bfloat16)  27.9 us
    all_gather x1, blocking collectives, body(): serve_router = lax.all_gather(row_router, 'ep', axis=1, tiled=True)  12.9 us
    all_to_all x1, starting transfers between devices, copy_for_each(): lax.all_to_all(jnp.broadcast_to(array[None], (size, *array.shape)), axis,...  11.3 us
    all_to_all x2, local copies, waits for them, and re-layouts, body(): lax.all_to_all(narrow_down, FSDP, split_axis=1, concat_axis=2, tiled=True)  8.73 us
    all_to_all x1, starting transfers between devices, body(): lax.all_to_all(narrow_down, FSDP, split_axis=1, concat_axis=2, tiled=True)  5.7 us
    convert_element_type x1, other arithmetic, body(): narrow_down = (w_down / jnp.expand_dims(scale_down, 2)).astype(jnp.bfloat16)  4.71 us
  transfers between devices with their start and end apart: 2, of which 1 were waited for; matrix products, arithmetic and copies ran while one was open for 22% of the time, Pallas kernels for 0%

commit v1 on v0

--- a/solution.py
+++ b/solution.py
@@ -40,7 +40,12 @@
     )
     part_router = (router_weight * router_gain[:, None]).astype(jnp.bfloat16)
     row_router = gather_directly(part_router, FSDP, 0)
-    serve_router = lax.all_gather(row_router, "ep", axis=1, tiled=True)
+    serve_router = jnp.concatenate(
+        jax.lax.all_to_all(
+            jnp.stack([row_router for _ in range(jax.lax.axis_size("ep"))], 0), "ep", 0, 0
+        ),
+        axis=1,
+    )
     return (serve_down, scale_down, serve_router)
 
 

time: 178 us -> 197 us (1.11); the launches traced: 178 us -> 194 us
  waiting for transfers between devices: 50.5 us -> 73.9 us
  blocking collectives: 60.9 us -> 47.9 us
  starting transfers between devices: 17 us -> 21.9 us
    all_to_all x1, waiting for transfers between devices: 50.5 us -> 73.9 us  [body(): lax.all_to_all(narrow_down, FSDP, split_axis=1, concat_axis=2, tiled=True)]
    all_gather x1 -> x0, blocking collectives: 12.9 us -> none  [body(): serve_router = lax.all_gather(row_router, 'ep', axis=1, tiled=True)]
    all_to_all x0 -> x1, starting transfers between devices: none -> 4.92 us  [body(): jax.lax.all_to_all(jnp.stack([row_router for _ in range(jax.lax.axis_size...]
  transfers between devices with their start and end apart: 2 -> 3, of which waited for: 1 -> 1; matrix products, arithmetic and copies ran while one was open for 22% -> 20% of each run, Pallas kernels for 0% -> 0%
where the time goes in v1:
time: 197 us; the launch traced here: 194 us
  waiting for transfers between devices  73.9 us (38%)
  blocking collectives  47.9 us (24%)
  local copies, waits for them, and re-layouts  39.4 us (20%)
  starting transfers between devices  21.9 us (11%)
  other arithmetic  10 us (5%)
    all_to_all x1, waiting for transfers between devices, body(): lax.all_to_all(narrow_down, FSDP, split_axis=1, concat_axis=2, tiled=True)  73.9 us
    psum x2, blocking collectives, by_axis(): array = lax.psum(array, axis)  47.9 us
    convert_element_type x1, local copies, waits for them, and re-layouts, body(): narrow_down = (w_down / jnp.expand_dims(scale_down, 2)).astype(jnp.bfloat16)  27.9 us
    all_to_all x1, starting transfers between devices, copy_for_each(): lax.all_to_all(jnp.broadcast_to(array[None], (size, *array.shape)), axis,...  11.3 us
    all_to_all x2, local copies, waits for them, and re-layouts, body(): lax.all_to_all(narrow_down, FSDP, split_axis=1, concat_axis=2, tiled=True)  8.73 us
    all_to_all x1, starting transfers between devices, body(): lax.all_to_all(narrow_down, FSDP, split_axis=1, concat_axis=2, tiled=True)  5.7 us
    all_to_all x1, starting transfers between devices, body(): jax.lax.all_to_all(jnp.stack([row_router for _ in range(jax.lax.axis_size...  4.92 us
    convert_element_type x1, other arithmetic, body(): narrow_down = (w_down / jnp.expand_dims(scale_down, 2)).astype(jnp.bfloat16)  4.7 us
  transfers between devices with their start and end apart: 3, of which 1 were waited for; matrix products, arithmetic and copies ran while one was open for 20% of the time, Pallas kernels for 0%

profile of v1, /device:TPU:8, one launch (start us, length us, event | category | flops | bytes accessed | tf_op | source)
XLA Modules:
  0.0 193.8 jit_solution(6161485286738521264)
XLA Ops:
  0.6 0.7 multiply_convert_fusion
  1.3 0.6 broadcast_in_dim.2
  1.9 11.3 %all-to-all-start.1 = ((bf16[32,128,2]{1,2,0:T(2,128)(2,1)}), bf16[32,128,2]{1,2,0:T(2,128)(2,1)S(1)}, u32[]{:S(2)}, u32[]{:S(2)}) async-start(bf16[32,128,2]{1,2,0:T(2,128)(2,1)} %broadcast_in_dim.2), calls=%async_computation.1 | async-start | bytes 32768 | tf_op jit(solution)/shard_map/all_to_all | solution.py:24
  13.3 4.6 %multiply_reduce_fusion = f32[2,6400]{1,0:T(2,128)S(1)} fusion(f32[2,6400,128]{2,1,0:T(8,128)} %param.3), kind=kLoop, calls=%fused_computation.1 | loop fusion | flops 3264000 | bytes 6604800 | tf_op jit(solution)/shard_map/reduce_sum | solution.py:34
  17.9 30.5 %psum.14 = f32[2,6400]{1,0:T(2,128)S(1)} all-reduce(f32[2,6400]{1,0:T(2,128)S(1)} %multiply_reduce_fusion), channel_id=1, replica_groups=mesh['ep'=8,'fsdp_0'=8,'fsdp_1'=4] {'fsdp_0'}, use_global_device_ids=true, to_apply=%region_1.0 | all-reduce | flops 12800 | bytes 102400 | tf_op jit(solution)/shard_map/psum | solution.py:12
  48.4 17.4 %psum.15 = f32[2,6400]{1,0:T(2,128)S(1)} all-reduce(f32[2,6400]{1,0:T(2,128)S(1)} %psum.14), channel_id=1, replica_groups=mesh['ep'=8,'fsdp_0'=8,'fsdp_1'=4] {'fsdp_1'}, use_global_device_ids=true, to_apply=%region_2.0 | all-reduce | flops 12800 | bytes 102400 | tf_op jit(solution)/shard_map/psum | solution.py:12
  65.8 0.1 sqrt.3
  65.9 0.0 all-to-all-done.1
  65.9 0.7 stack.3
  66.6 4.9 %all-to-all-start.2 = ((bf16[8,4096,2]{1,2,0:T(2,128)(2,1)}), bf16[8,4096,2]{1,2,0:T(2,128)(2,1)S(1)}, u32[]{:S(2)}, u32[]{:S(2)}) async-start(bf16[8,4096,2]{1,2,0:T(2,128)(2,1)} %stack.3), calls=%async_computation.2 | async-start | bytes 262144 | tf_op jit(solution)/shard_map/all_to_all | solution.py:44
  71.6 4.7 %divide_convert_fusion = bf16[2,6400,128]{2,1,0:T(8,128)(2,1)S(1)} fusion(f32[2,6400,128]{2,1,0:T(8,128)} %param.3, f32[2,6400]{1,0:T(2,128)S(1)} %sqrt.3), kind=kLoop, calls=%fused_computation | loop fusion | flops 3276800 | bytes 9881600 | tf_op jit(solution)/shard_map/convert_element_type | solution.py:36
  76.3 27.9 %copy.10 = bf16[2,6400,128]{2,0,1:T(2,128)(2,1)} copy(bf16[2,6400,128]{2,1,0:T(8,128)(2,1)S(1)} %divide_convert_fusion) | data formatting | bytes 6553600 | tf_op jit(solution)/shard_map/convert_element_type | solution.py:36
  104.1 0.0 all-to-all-done.2
  104.1 5.7 %all-to-all-start = ((bf16[2,6400,128]{2,0,1:T(2,128)(2,1)}), bf16[2,6400,128]{2,0,1:T(2,128)(2,1)S(1)}, u32[]{:S(2)}, u32[]{:S(2)}) async-start(bf16[2,6400,128]{2,0,1:T(2,128)(2,1)} %copy.10), calls=%async_computation | async-start | bytes 6553600 | tf_op jit(solution)/shard_map/all_to_all | solution.py:37
  109.9 0.7 constant_dynamic-slice_fusion
  110.5 0.7 reshape.18
  111.2 73.9 %all-to-all-done = bf16[2,6400,128]{2,0,1:T(2,128)(2,1)S(1)} async-done(((bf16[2,6400,128]{2,0,1:T(2,128)(2,1)}), bf16[2,6400,128]{2,0,1:T(2,128)(2,1)S(1)}, u32[]{:S(2)}, u32[]{:S(2)}) %all-to-all-start) | async-done | bytes 3276832 | tf_op jit(solution)/shard_map/all_to_all | solution.py:37
  185.1 2.5 %copy.11 = bf16[2,200,32,128]{3,2,1,0:T(8,128)(2,1)} copy(bf16[2,200,32,128]{3,0,1,2:T(2,128)(2,1)S(1)} %bitcast.9) | data formatting | bytes 6553600 | tf_op jit(solution)/shard_map/all_to_all | solution.py:37
  187.6 6.2 %all_to_all.22 = bf16[2,200,4096]{2,1,0:T(8,128)(2,1)} reshape(bf16[2,200,32,128]{3,2,1,0:T(8,128)(2,1)} %copy.11) | data formatting | bytes 6553600 | tf_op jit(solution)/shard_map/all_to_all | solution.py:37
Async XLA Ops:
  1.9 64.0 %all-to-all-start.1 = ((bf16[32,128,2]{1,2,0:T(2,128)(2,1)}), bf16[32,128,2]{1,2,0:T(2,128)(2,1)S(1)}, u32[]{:S(2)}, u32[]{:S(2)}) async-start(bf16[32,128,2]{1,2,0:T(2,128)(2,1)} %broadcast_in_dim.2), calls=%async_computation.1 | async-start | bytes 32768 | tf_op jit(solution)/shard_map/all_to_all | solution.py:24
  66.6 37.5 %all-to-all-start.2 = ((bf16[8,4096,2]{1,2,0:T(2,128)(2,1)}), bf16[8,4096,2]{1,2,0:T(2,128)(2,1)S(1)}, u32[]{:S(2)}, u32[]{:S(2)}) async-start(bf16[8,4096,2]{1,2,0:T(2,128)(2,1)} %stack.3), calls=%async_computation.2 | async-start | bytes 262144 | tf_op jit(solution)/shard_map/all_to_all | solution.py:44
  104.1 81.0 %all-to-all-start = ((bf16[2,6400,128]{2,0,1:T(2,128)(2,1)}), bf16[2,6400,128]{2,0,1:T(2,128)(2,1)S(1)}, u32[]{:S(2)}, u32[]{:S(2)}) async-start(bf16[2,6400,128]{2,0,1:T(2,128)(2,1)} %copy.10), calls=%async_computation | async-start | bytes 6553600 | tf_op jit(solution)/shard_map/all_to_all | solution.py:37
